TPU v7x, 32 devices: a whole 2x2x4 slice. The times are simulated.
32 devices in a mesh: seq: 16 (over z, y, x), head: 2 (over core).
Axes of the slice: x: 2, y: 2, z: 4, core: 2. Of those that a mesh axis runs over, the one named last changes fastest.
Arguments:
- acceptance_signal: bfloat16 [8192, 2048], P(('seq', 'head')), may hold values from -6 to 6
- lookup_entries: bfloat16 [8192, 2048], P(('seq', 'head')), may hold values from -6 to 6
- content_entries: bfloat16 [8192, 2048], P(('seq', 'head')), may hold values from -6 to 6
- fading_exponent_table: bfloat16 [8192, 2048], P(('seq', 'head')), may hold values from -17 to 0
- raw_control_signal: bfloat16 [8192, 2048], P(('seq', 'head')), may hold values from -6 to 6
- current_token_reward: float32 [32, 64], P('head'), may hold values from -1 to 1
- slice_scaling_factor: float32 [2048], P('head'), may hold values from 0.1 to 1.9
- result_mapping: bfloat16 [2048, 4096], P('head'), may hold values from -0.125 to 0.125
Outputs:
- time_mixed: bfloat16 [8192, 4096], P(('seq', 'head'))
All inputs are finite; a program needn't handle non-finite values.
Results may differ from a plain program's by a relative error of at most 0.009.
Values may be sent and summed in bfloat16 or wider, within the bound.
A program may use at most 192 MiB of HBM per device.

v0:
```python
import jax
import jax.numpy as jnp
from jax import lax
from jax.sharding import PartitionSpec as P

BLOCK = 128


EPS = 1e-05


def shards(
    acceptance_signal,
    lookup_entries,
    content_entries,
    fading_exponent_table,
    raw_control_signal,
    current_token_reward,
    slice_scaling_factor,
    result_mapping,
):
    high = lax.Precision.HIGHEST
    slices_for_each_chip = current_token_reward.shape[0]
    slice_breadth = current_token_reward.shape[1]
    width_dev = slices_for_each_chip * slice_breadth
    rec_t, key_t, val_t, logit_t, gate_t = (
        lax.all_to_all(acceptance_signal, "head", split_axis=1, concat_axis=0, tiled=True),
        lax.all_to_all(lookup_entries, "head", split_axis=1, concat_axis=0, tiled=True),
        lax.all_to_all(content_entries, "head", split_axis=1, concat_axis=0, tiled=True),
        lax.all_to_all(fading_exponent_table, "head", split_axis=1, concat_axis=0, tiled=True),
        lax.all_to_all(raw_control_signal, "head", split_axis=1, concat_axis=0, tiled=True),
    )
    tokens = rec_t.shape[0]
    blocks = tokens // BLOCK
    shape4 = (blocks, BLOCK, slices_for_each_chip, slice_breadth)

    def head_major(values):
        return jnp.transpose(values.reshape(shape4), (0, 2, 1, 3))

    acceptance_single_real = head_major(rec_t).astype(jnp.float32)
    lookup_single_real = head_major(key_t).astype(jnp.float32)
    content_single_real = head_major(val_t).astype(jnp.float32)
    log_decay = -jnp.exp(head_major(logit_t).astype(jnp.float32))
    cum_incl = jnp.cumsum(log_decay, axis=2)
    cum_excl = cum_incl - log_decay
    block_total = cum_incl[:, :, -1]
    rec_scaled = acceptance_single_real * jnp.exp(cum_excl)
    key_scaled = lookup_single_real * jnp.exp(-cum_incl)
    key_ending = lookup_single_real * jnp.exp(block_total[:, :, None] - cum_incl)
    positions = jnp.arange(BLOCK)
    strict = (positions[:, None] > positions[None, :]).astype(jnp.float32)
    scores = jnp.einsum("nhti,nhsi->nhts", rec_scaled, key_scaled, precision=high) * strict
    within = jnp.einsum("nhts,nhsj->nhtj", scores, content_single_real, precision=high)
    reward = current_token_reward[None, :, None, :]
    diagonal_contribution = (
        jnp.sum(acceptance_single_real * reward * lookup_single_real, axis=-1, keepdims=True)
        * content_single_real
    )
    block_states = jnp.einsum("nhsi,nhsj->nhij", key_ending, content_single_real, precision=high)
    block_decay = jnp.exp(block_total)

    def advance(state, inputs):
        decay, contrib = inputs
        return (decay[..., None] * state + contrib, state)

    empty = jnp.zeros((slices_for_each_chip, slice_breadth, slice_breadth), jnp.float32)
    local_state, entering = lax.scan(advance, empty, (block_decay, block_states))
    device_log = jnp.sum(block_total, axis=0)
    all_log, all_state = (
        lax.all_gather(device_log[None], "seq", axis=0, tiled=True),
        lax.all_gather(local_state[None], "seq", axis=0, tiled=True),
    )
    mine = lax.axis_index("seq")
    group_ids = jnp.arange(all_log.shape[0], dtype=jnp.int32)
    running = jnp.cumsum(all_log, axis=0)
    picker = (group_ids == mine - 1).astype(jnp.float32)[:, None, None]
    reached = jnp.sum(picker * running, axis=0)
    earlier = (group_ids < mine)[:, None, None]
    exponent = jnp.where(earlier, reached[None] - running, 0.0)
    weights = jnp.where(earlier, jnp.exp(exponent), 0.0)
    carried = jnp.einsum("ghi,ghij->hij", weights, all_state, precision=high)
    prior_decay = jnp.exp(jnp.cumsum(block_total, axis=0) - block_total)
    entering = entering + prior_decay[..., None] * carried[None]
    across = jnp.einsum("nhti,nhij->nhtj", rec_scaled, entering, precision=high)
    output = within + diagonal_contribution + across
    mean = jnp.mean(output, axis=-1, keepdims=True)
    centred = output - mean
    var = jnp.mean(centred * centred, axis=-1, keepdims=True)
    gain = slice_scaling_factor.reshape(slices_for_each_chip, slice_breadth)[None, :, None, :]
    normed = centred / jnp.sqrt(var + EPS) * gain
    gate_heads = head_major(gate_t).astype(jnp.float32)
    gated_heads = (normed * jax.nn.silu(gate_heads)).astype(jnp.bfloat16)
    gated = jnp.transpose(gated_heads, (0, 2, 1, 3)).reshape(tokens, width_dev)
    return lax.psum_scatter(
        jnp.dot(gated, result_mapping, preferred_element_type=jnp.float32).astype(jnp.bfloat16),
        "head",
        scatter_dimension=0,
        tiled=True,
    )


def solution(mesh):
    placed = (
        P(("seq", "head"), None),
        P(("seq", "head"), None),
        P(("seq", "head"), None),
        P(("seq", "head"), None),
        P(("seq", "head"), None),
        P("head", None),
        P("head"),
        P("head", None),
    )
    return jax.shard_map(
        shards, mesh=mesh, in_specs=placed, out_specs=P(("seq", "head"), None), check_vma=False
    )
```

profile of v0, /device:TPU:0, one launch (start us, length us, event | category | flops | bytes accessed | tf_op | source)
XLA Modules:
  0.0 250.9 jit_solution(18437913473303088898)
XLA Ops:
  6.5 2.3 copy.34
  8.9 3.6 %all-to-all-start.1 = ((bf16[256,2,1024]{0,2,1:T(8,128)(2,1)}), bf16[256,2,1024]{0,2,1:T(8,128)(2,1)S(1)}, u32[]{:S(2)}, u32[]{:S(2)}) async-start(bf16[256,2,1024]{0,2,1:T(8,128)(2,1)} %bitcast.3), calls=%async_computation.1 | async-start | bytes 2097152 | tf_op jit(solution)/shard_map/all_to_all | solution.py:30
  12.5 1.3 copy.31
  13.8 0.8 all-to-all-done.1
  14.6 3.6 %all-to-all-start = ((bf16[256,2,1024]{0,2,1:T(8,128)(2,1)}), bf16[256,2,1024]{0,2,1:T(8,128)(2,1)S(1)}, u32[]{:S(2)}, u32[]{:S(2)}) async-start(bf16[256,2,1024]{0,2,1:T(8,128)(2,1)} %bitcast.106), calls=%async_computation | async-start | bytes 2097152 | tf_op jit(solution)/shard_map/all_to_all | solution.py:27
  18.2 1.6 negate_bitcast_fusion
  19.8 2.9 %copy.61 = f32[2,256,1024]{2,1,0:T(8,128)} copy(f32[2,256,1024]{1,2,0:T(8,128)} %negate_bitcast_fusion) | data formatting | bytes 4194304 | tf_op jit(solution)/shard_map/neg | solution.py:43
  22.7 4.5 %reshape.103 = f32[4,128,16,64]{3,2,1,0:T(8,128)} reshape(f32[2,256,1024]{2,1,0:T(8,128)} %copy.61) | data formatting | bytes 4194304 | tf_op jit(solution)/shard_map/neg | solution.py:43
  27.2 2.6 %fusion.3 = f32[4,16,128,64]{3,1,2,0:T(8,128)S(1)} fusion(f32[4,128,16,64]{3,2,1,0:T(8,128)} %reshape.103), kind=kOutput, calls=%fused_computation.11 | output fusion | flops 66584576 | bytes 4194304 | tf_op jit(solution)/shard_map/jit(cumsum)/reduce_window_sum | solution.py:44
  29.9 1.9 copy-done.3
  31.8 1.4 copy.37
  33.2 3.6 %all-to-all-start.2 = ((bf16[256,2,1024]{0,2,1:T(8,128)(2,1)}), bf16[256,2,1024]{0,2,1:T(8,128)(2,1)S(1)}, u32[]{:S(2)}, u32[]{:S(2)}) async-start(bf16[256,2,1024]{0,2,1:T(8,128)(2,1)} %bitcast.108), calls=%async_computation.2 | async-start | bytes 2097152 | tf_op jit(solution)/shard_map/all_to_all | solution.py:28
  36.8 1.5 convert_bitcast_fusion.1
  38.3 3.0 %copy.60 = f32[2,256,1024]{2,1,0:T(8,128)} copy(f32[2,256,1024]{1,2,0:T(8,128)} %convert_bitcast_fusion.1) | data formatting | bytes 4194304 | tf_op jit(solution)/shard_map/convert_element_type | solution.py:40
  41.3 1.3 copy.42
  42.6 3.6 %all-to-all-start.3 = ((bf16[256,2,1024]{0,2,1:T(8,128)(2,1)}), bf16[256,2,1024]{0,2,1:T(8,128)(2,1)S(1)}, u32[]{:S(2)}, u32[]{:S(2)}) async-start(bf16[256,2,1024]{0,2,1:T(8,128)(2,1)} %bitcast.9), calls=%async_computation.3 | async-start | bytes 2097152 | tf_op jit(solution)/shard_map/all_to_all | solution.py:29
  46.2 0.6 all-gather.4.cloned.1.call-start
  46.8 1.5 convert_bitcast_fusion
  48.3 2.9 %copy.62 = f32[2,256,1024]{2,1,0:T(8,128)} copy(f32[2,256,1024]{1,2,0:T(8,128)} %convert_bitcast_fusion) | data formatting | bytes 4194304 | tf_op jit(solution)/shard_map/convert_element_type | solution.py:41
  51.2 1.1 copy.43
  52.3 0.7 reshape.93
  53.0 4.5 %reshape.104 = f32[4,128,16,64]{3,2,1,0:T(8,128)} reshape(f32[2,256,1024]{2,1,0:T(8,128)} %copy.62) | data formatting | bytes 4194304 | tf_op jit(solution)/shard_map/convert_element_type | solution.py:41
  57.5 4.5 %reshape.102 = f32[4,128,16,64]{3,2,1,0:T(8,128)} reshape(f32[2,256,1024]{2,1,0:T(8,128)} %copy.60) | data formatting | bytes 4194304 | tf_op jit(solution)/shard_map/convert_element_type | solution.py:40
  62.1 9.7 %fusion.2 = (f32[4,16,128]{1,2,0:T(8,128)S(1)}, f32[4,16,128,64]{3,1,2,0:T(8,128)}, f32[4,16,128,64]{3,1,2,0:T(8,128)S(1)}, f32[4,16,128,64]{3,1,2,0:T(8,128)}) fusion(f32[4,128,16,64]{3,2,1,0:T(8,128)} %reshape.104, f32[4,128,16,64]{3,2,1,0:T(8,128)} %reshape.102, f32[16,64]{1,0:T(8,128)S(1)} %copy-done.10, f32[4,16,128,64]{3,1,2,0:T(8,128)} %copy-done.3, ...), kind=kLoop, calls=%fused_computation.9 | loop fusion | flops 4710400 | bytes 14733312 | tf_op jit(solution)/shard_map/reduce_sum | solution.py:56
  71.7 5.4 %fusion.7 = f32[4,16,64,64]{3,2,1,0:T(8,128)} fusion(f32[4,16,128,64]{3,1,2,0:T(8,128)S(1)} %get-tuple-element.67, bf16[4,128,16,64]{1,0,3,2:T(4,128)(2,1)S(1)} %reshape.93), kind=kOutput, calls=%fused_computation.16 | convolution fusion | flops 402653184 | bytes 4194304 | tf_op jit(solution)/shard_map/nhsi,nhsj->nhij/dot_general | solution.py:59
  77.1 8.8 %while.13 = (s32[]{:T(128)}, f32[16,64,64]{2,1,0:T(8,128)S(1)}, f32[4,16,64,64]{3,2,1,0:T(8,128)}, f32[4,16,64]{2,1,0:T(8,128)S(1)}, f32[4,16,64,64]{3,2,1,0:T(8,128)}, /*index=5*/s32[]{:T(128)}, s32[]{:T(128)}) while((s32[]{:T(128)}, f32[16,64,64]{2,1,0:T(8,128)S(1)}, f32[4,16,64,64]{3,2,1,0:T(8,128)}, ...), condition=%wide.region_3.4_spmd.clone, body=%wide.region_2.3_spmd.clone.sunk | while | flops 262147 | bytes 1585260 | solution.py:67
  77.1 0.8 bitcast_dynamic-update-slice_fusion.2
  78.0 1.3 bitcast_add_fusion.4
  79.3 0.8 bitcast_dynamic-update-slice_fusion.2
  80.2 1.3 bitcast_add_fusion.4
  81.5 0.9 bitcast_dynamic-update-slice_fusion.2
  82.4 1.3 bitcast_add_fusion.4
  83.8 0.8 bitcast_dynamic-update-slice_fusion.2
  84.6 1.3 bitcast_add_fusion.4
  86.0 0.8 copy-done
  86.8 0.0 all-gather.4.cloned.1.call-update
  86.8 1.3 copy.51
  88.1 3.6 %all-to-all-start.4 = ((bf16[256,2,1024]{0,2,1:T(8,128)(2,1)}), bf16[256,2,1024]{0,2,1:T(8,128)(2,1)S(1)}, u32[]{:S(2)}, u32[]{:S(2)}) async-start(bf16[256,2,1024]{0,2,1:T(8,128)(2,1)} %bitcast.23), calls=%async_computation.4 | async-start | bytes 2097152 | tf_op jit(solution)/shard_map/all_to_all | solution.py:31
  91.7 0.2 reduce-scatter.2.cloned.1.call-start
  92.0 0.1 mul.116
  92.0 1.8 all-to-all-done.4
  93.8 0.2 convert_bitcast_fusion.2
  94.0 1.6 copy.52
  95.6 3.0 %reshape.95 = f32[4,128,16,64]{1,0,3,2:T(4,128)} reshape(f32[2,256,1024]{1,0,2:T(2,128)S(1)} %copy.52) | data formatting | bytes 4194304 | tf_op jit(solution)/shard_map/convert_element_type | solution.py:91
  98.7 3.2 %copy.40 = f32[4,16,128,64]{2,3,1,0:T(8,128)S(1)} copy(f32[4,16,128,64]{3,1,2,0:T(8,128)} %get-tuple-element.66) | data formatting | bytes 4194304 | tf_op jit(solution)/shard_map/mul | solution.py:47
  101.9 0.1 copy.50
  102.0 0.1 copy.45
  102.1 44.8 %all-gather = f32[256,64]{1,0:T(8,128)S(1)} all-gather(f32[16,64]{1,0:T(8,128)S(1)} %get-tuple-element.69), channel_id=2, replica_groups=mesh['seq'=16,'head'=2] {'seq'}, dimensions={0}, use_global_device_ids=true | all-gather | bytes 69632 | tf_op jit(solution)/shard_map/all_gather | solution.py:70
  146.9 0.7 fusion.35
  147.6 0.1 multiply_reduce_fusion.1
  147.7 0.1 select_bitcast_fusion
  147.8 1.0 copy.56
  148.8 0.9 fusion.22
  149.7 11.8 %fusion.9 = f32[4,16,128,128]{3,2,1,0:T(8,128)S(1)} fusion(f32[4,16,128,64]{2,3,1,0:T(8,128)S(1)} %copy.40, f32[4,16,128,64]{3,1,2,0:T(8,128)} %get-tuple-element.68), kind=kOutput, calls=%fused_computation.18 | convolution fusion | flops 805306368 | bytes 8388608 | tf_op jit(solution)/shard_map/nhti,nhsi->nhts/dot_general | solution.py:52
  161.5 4.4 %fusion.11 = f32[4,16,128,64]{2,3,1,0:T(8,128)S(1)} fusion(f32[4,16,128,128]{3,2,1,0:T(8,128)S(1)} %fusion.9, f32[128,128]{1,0:T(8,128)S(1)} %fusion.31, bf16[4,128,16,64]{1,0,3,2:T(4,128)(2,1)S(1)} %reshape.93), kind=kOutput, calls=%fused_computation.20 | convolution fusion | flops 806354944 | bytes 7405568 | tf_op jit(solution)/shard_map/nhts,nhsj->nhtj/dot_general | solution.py:53
  165.9 37.7 %all-gather.4.cloned.1.call-done = f32[256,64,64]{2,1,0:T(8,128)} async-done(((f32[16,64,64]{2,1,0:T(8,128)}), f32[256,64,64]{2,1,0:T(8,128)}) %all-gather.4.cloned.1.call-update) | async-done | bytes 4194320 | tf_op jit(solution)/shard_map/all_gather | solution.py:71
  203.6 15.6 %fusion = f32[16,64,1,64]{3,2,1,0:T(1,128)S(1)} fusion(f32[16,16,64,1]{0,3,2,1:T(1,128)} %copy.56, f32[16,16,64,64]{3,2,1,0:T(8,128)} %bitcast.105), kind=kOutput, calls=%fused_computation.3 | convolution fusion | flops 12582912 | bytes 4521984 | tf_op jit(solution)/shard_map/ghi,ghij->hij/dot_general | solution.py:81
  219.2 4.2 %fusion.32 = (f32[4,16,128]{2,1,0:T(8,128)S(1)}, f32[4,16,128,64]{2,3,1,0:T(8,128)S(1)}) fusion(f32[4,16,128,64]{2,3,1,0:T(8,128)S(1)} %fusion.11, bf16[4,128,16,64]{1,0,3,2:T(4,128)(2,1)S(1)} %reshape.93, f32[4,16,128]{2,1,0:T(8,128)S(1)} %copy.50, f32[4,16,128,64]{2,3,1,0:T(8,128)S(1)} %copy-done.2, f32[4,16,64,64]{3,2,1,0:T(8,128)S(1)} %copy-done.5, ...), kind=kOutput, calls=%fused_computation.57 | convolution fusion | flops 405790720 | bytes 8732672 | tf_op jit(solution)/shard_map/nhti,nhij->nhtj/dot_general | solution.py:84
  223.4 0.9 multiply_reduce_fusion
  224.3 0.7 copy-done.4
  225.0 1.1 fusion.21
  226.1 0.9 copy.55
  227.1 6.3 %convolution_convert_fusion = bf16[512,4096]{1,0:T(8,128)(2,1)} fusion(bf16[1024,4096]{1,0:T(8,128)(2,1)S(1)} %bitcast.114, bf16[128,8,4,128]{3,2,1,0:T(4,128)(2,1)S(1)} %bitcast.111), kind=kOutput, calls=%fused_computation.5 | convolution fusion | flops 4297064448 | bytes 13631488 | tf_op jit(solution)/shard_map/dot_general | solution.py:95
  233.4 10.4 %reduce-scatter.2.cloned.1.call-done = bf16[256,4096]{1,0:T(8,128)(2,1)} async-done(((bf16[512,4096]{1,0:T(8,128)(2,1)}), bf16[256,4096]{1,0:T(8,128)(2,1)}) %reduce-scatter.2.cloned.1.call-update) | async-done | bytes 2097168 | tf_op jit(solution)/shard_map/reduce_scatter | solution.py:94
  (43 shorter events, 0.2 us)
Async XLA Ops:
  6.5 6.0 %copy-start.6 = (bf16[256,2048]{1,0:T(8,128)(2,1)S(1)}, bf16[256,2048]{1,0:T(8,128)(2,1)}, u32[]{:S(2)}) copy-start(bf16[256,2048]{1,0:T(8,128)(2,1)} %param.10) | copy-start | bytes 3145732
  8.9 5.7 %all-to-all-start.1 = ((bf16[256,2,1024]{0,2,1:T(8,128)(2,1)}), bf16[256,2,1024]{0,2,1:T(8,128)(2,1)S(1)}, u32[]{:S(2)}, u32[]{:S(2)}) async-start(bf16[256,2,1024]{0,2,1:T(8,128)(2,1)} %bitcast.3), calls=%async_computation.1 | async-start | bytes 2097152 | tf_op jit(solution)/shard_map/all_to_all | solution.py:30
  14.6 18.6 %all-to-all-start = ((bf16[256,2,1024]{0,2,1:T(8,128)(2,1)}), bf16[256,2,1024]{0,2,1:T(8,128)(2,1)S(1)}, u32[]{:S(2)}, u32[]{:S(2)}) async-start(bf16[256,2,1024]{0,2,1:T(8,128)(2,1)} %bitcast.106), calls=%async_computation | async-start | bytes 2097152 | tf_op jit(solution)/shard_map/all_to_all | solution.py:27
  27.2 4.6 %copy-start.7 = (bf16[256,2048]{1,0:T(8,128)(2,1)S(1)}, bf16[256,2048]{1,0:T(8,128)(2,1)}, u32[]{:S(2)}) copy-start(bf16[256,2048]{1,0:T(8,128)(2,1)} %param.11) | copy-start | bytes 3145732
  29.8 2.0 copy-start.3
  33.2 9.4 %all-to-all-start.2 = ((bf16[256,2,1024]{0,2,1:T(8,128)(2,1)}), bf16[256,2,1024]{0,2,1:T(8,128)(2,1)S(1)}, u32[]{:S(2)}, u32[]{:S(2)}) async-start(bf16[256,2,1024]{0,2,1:T(8,128)(2,1)} %bitcast.108), calls=%async_computation.2 | async-start | bytes 2097152 | tf_op jit(solution)/shard_map/all_to_all | solution.py:28
  38.3 3.0 %copy-start.8 = (bf16[256,2048]{1,0:T(8,128)(2,1)S(1)}, bf16[256,2048]{1,0:T(8,128)(2,1)}, u32[]{:S(2)}) copy-start(bf16[256,2048]{1,0:T(8,128)(2,1)} %param.12) | copy-start | bytes 3145732
  42.6 8.6 %all-to-all-start.3 = ((bf16[256,2,1024]{0,2,1:T(8,128)(2,1)}), bf16[256,2,1024]{0,2,1:T(8,128)(2,1)S(1)}, u32[]{:S(2)}, u32[]{:S(2)}) async-start(bf16[256,2,1024]{0,2,1:T(8,128)(2,1)} %bitcast.9), calls=%async_computation.3 | async-start | bytes 2097152 | tf_op jit(solution)/shard_map/all_to_all | solution.py:29
  46.2 157.4 %all-gather.4.cloned.1.call-start = ((), (), s32[]{:S(2)}) async-start(), calls=%async_computation.7 | async-start | bytes 8912896 | tf_op jit(solution)/shard_map/all_gather | solution.py:71
  57.5 4.5 %copy-start.10 = (f32[16,64]{1,0:T(8,128)S(1)}, f32[16,64]{1,0:T(8,128)}, u32[]{:S(2)}) copy-start(f32[16,64]{1,0:T(8,128)} %param.15) | copy-start | bytes 12292
  77.1 9.7 %copy-start.9 = (bf16[256,2048]{1,0:T(8,128)(2,1)S(1)}, bf16[256,2048]{1,0:T(8,128)(2,1)}, u32[]{:S(2)}) copy-start(bf16[256,2048]{1,0:T(8,128)(2,1)} %param.14) | copy-start | bytes 3145732
  86.0 0.8 copy-start
  86.8 5.1 %copy-start.11 = (f32[1024]{0:T(1024)S(1)}, f32[1024]{0:T(1024)}, u32[]{:S(2)}) copy-start(f32[1024]{0:T(1024)} %param.16) | copy-start | bytes 12292
  88.1 5.7 %all-to-all-start.4 = ((bf16[256,2,1024]{0,2,1:T(8,128)(2,1)}), bf16[256,2,1024]{0,2,1:T(8,128)(2,1)S(1)}, u32[]{:S(2)}, u32[]{:S(2)}) async-start(bf16[256,2,1024]{0,2,1:T(8,128)(2,1)} %bitcast.23), calls=%async_computation.4 | async-start | bytes 2097152 | tf_op jit(solution)/shard_map/all_to_all | solution.py:31
  91.7 152.1 %reduce-scatter.2.cloned.1.call-start = ((), (), s32[]{:S(2)}) async-start(), calls=%async_computation.6 | async-start | bytes 6291456 | tf_op jit(solution)/shard_map/reduce_scatter | solution.py:94
  101.9 47.8 %copy-start.1 = (f32[4,16,128,64]{2,3,1,0:T(8,128)}, f32[4,16,128,64]{2,3,1,0:T(8,128)S(1)}, u32[]{:S(2)}) copy-start(f32[4,16,128,64]{2,3,1,0:T(8,128)S(1)} %copy.40) | copy-start | bytes 6291460
  203.6 15.6 %copy-start.2 = (f32[4,16,128,64]{2,3,1,0:T(8,128)S(1)}, f32[4,16,128,64]{2,3,1,0:T(8,128)}, u32[]{:S(2)}) copy-start(f32[4,16,128,64]{2,3,1,0:T(8,128)} %copy-done.1) | copy-start | bytes 6291460
  203.6 15.6 %copy-start.5 = (f32[4,16,64,64]{3,2,1,0:T(8,128)S(1)}, f32[4,16,64,64]{3,2,1,0:T(8,128)}, u32[]{:S(2)}) copy-start(f32[4,16,64,64]{3,2,1,0:T(8,128)} %get-tuple-element.33) | copy-start | bytes 3145732
  219.2 7.9 %slice-start = ((s8[8388608]{0:T(1024)(128)(4,1)}), s8[4194304]{0:T(1024)(128)(4,1)S(1)}, s32[]{:S(2)}) async-start(s8[8388608]{0:T(1024)(128)(4,1)} %bitcast.113), calls=%async_computation.8 | async-start | bytes 8388608
  223.4 1.6 copy-start.4
  223.4 3.6 %slice-start.1 = ((s8[8388608]{0:T(1024)(128)(4,1)}), s8[4194304]{0:T(1024)(128)(4,1)S(1)}, s32[]{:S(2)}) async-start(s8[8388608]{0:T(1024)(128)(4,1)} %bitcast.113), calls=%async_computation.9 | async-start | bytes 8388608
Sparse Core Ops, SparseCore 0:
  86.9 116.6 all-gather.3
  233.6 10.2 reduce-scatter.1
where the time goes:
time: 255 us; the launch traced here: 251 us
  waiting for transfers between devices  50.6 us (20%)
  matrix products  47.7 us (19%)
  local copies, waits for them, and re-layouts  45.4 us (18%)
  blocking collectives  44.8 us (18%)
  other arithmetic  29.5 us (12%)
  starting transfers between devices  18.7 us (7%)
  between operations  14 us (5%)
    all_gather x1, blocking collectives, shards(): lax.all_gather(device_log[None], 'seq', axis=0, tiled=True)  44.8 us
    all_gather x1, waiting for transfers between devices, shards(): lax.all_gather(local_state[None], 'seq', axis=0, tiled=True)  37.7 us
    dot_general x1, matrix products, shards(): carried = jnp.einsum('ghi,ghij->hij', weights, all_state, precision=high)  15.6 us
    dot_general x1, matrix products, shards(): jnp.einsum('nhti,nhsi->nhts', rec_scaled, key_scaled, precision=high)  11.8 us
    unnamed x33, local copies, waits for them, and re-layouts  11.2 us
    reduce_scatter x1, waiting for transfers between devices, shards(): lax.psum_scatter(jnp.dot(gated, result_mapping, preferred_element_type=jn...  10.4 us
    reduce_sum x1, other arithmetic, shards(): jnp.sum(acceptance_single_real * reward * lookup_single_real, axis=-1, ke...  9.66 us
    convert_element_type x2, local copies, waits for them, and re-layouts, shards(): acceptance_single_real = head_major(rec_t).astype(jnp.float32)  7.54 us
  transfers between devices with their start and end apart: 7, of which 4 were waited for; matrix products, arithmetic and copies ran while one was open for 21% of the time, Pallas kernels for 0%

commit v1 on v0

v1 whole, which is shorter than its diff:
```python
import functools

import jax
import jax.numpy as jnp
from jax import lax
from jax.experimental import pallas as pl
from jax.experimental.pallas import tpu as pltpu
from jax.sharding import PartitionSpec as P

BLOCK = 128
LANES = 128
QUAD = 256
CHUNK = 512
EPS = 1e-05
MESH = pl.DeviceIdType.MESH
F32 = jnp.float32
BF16 = jnp.bfloat16


def dot(a, b):
    return jnp.dot(a, b, preferred_element_type=F32)


def dot_nt(a, b):
    return lax.dot_general(a, b, (((1,), (1,)), ((), ())), preferred_element_type=F32)


def dot_tn(a, b):
    return lax.dot_general(a, b, (((0,), (0,)), ((), ())), preferred_element_type=F32)


def split_heads(x, low):
    zero = jnp.zeros_like(x)
    return jnp.concatenate([jnp.where(low, x, zero), jnp.where(low, zero, x)], axis=0)


def kernel(
    n, breadth,
    rec_hbm, key_hbm, val_hbm, fade_hbm, gate_hbm, reward_ref, gain_ref, map_hbm,
    out_hbm,
    fade, key, val, rec, gate, weight, rec_mid, key_mid, local_out, entering, pref_row, mid_row,
    outbox, outdec, inbox, indec, outbox2, carry, gated, snd, rcv, outv,
    in_send, in_recv, in_local, w_sem, s_send, s_recv, d_send, d_recv, c_send, c_recv,
    p_send, p_recv, o_sem,
):
    me, core = lax.axis_index("seq"), lax.axis_index("head")
    other = 1 - core
    rows, width = rec_hbm.shape[0], rec.shape[1]
    tokens = rec.shape[0]
    blocks, quads, pairs = tokens // BLOCK, width // QUAD, width // LANES
    chunks = weight.shape[0]
    piece = outbox.shape[1]
    per_pair = breadth // piece
    my_rows = pl.ds(pl.multiple_of(core * rows, 128), rows)
    their_rows = pl.ds(pl.multiple_of(other * rows, 128), rows)
    my_cols = pl.ds(pl.multiple_of(core * width, 128), width)
    their_cols = pl.ds(pl.multiple_of(other * width, 128), width)
    pairs_io = ((fade_hbm, fade), (key_hbm, key), (val_hbm, val), (rec_hbm, rec), (gate_hbm, gate))

    locals_ = [
        pltpu.make_async_copy(src.at[:, my_cols], dst.at[my_rows, :], in_local.at[i])
        for i, (src, dst) in enumerate(pairs_io)
    ]
    remotes = [
        pltpu.make_async_remote_copy(
            src_ref=src.at[:, their_cols], dst_ref=dst.at[my_rows, :],
            send_sem=in_send.at[i], recv_sem=in_recv.at[i],
            device_id=(me, other), device_id_type=MESH,
        )
        for i, (src, dst) in enumerate(pairs_io)
    ]
    barrier = pltpu.get_barrier_semaphore()
    pl.semaphore_signal(barrier, inc=1, device_id=(me, other), device_id_type=MESH)

    def greet(d, c):
        pl.semaphore_signal(
            barrier, inc=1, device_id=(lax.rem(me + d, n), core), device_id_type=MESH
        )
        return c

    lax.fori_loop(1, n, greet, 0)
    for copy in locals_:
        copy.start()
    pl.semaphore_wait(barrier, n)
    for copy in remotes:
        copy.start()

    def weight_copy(c):
        return pltpu.make_async_copy(
            map_hbm.at[:, pl.ds(pl.multiple_of(c * CHUNK, CHUNK), CHUNK)], weight.at[c], w_sem.at[c]
        )

    for c in range(chunks):
        weight_copy(c).start()

    t_id = lax.broadcasted_iota(jnp.int32, (BLOCK, 2 * BLOCK), 0)
    s_id = lax.rem(lax.broadcasted_iota(jnp.int32, (BLOCK, 2 * BLOCK), 1), BLOCK)
    incl = jnp.where(t_id >= s_id, 1.0, 0.0).astype(BF16)
    low = lax.broadcasted_iota(jnp.int32, (BLOCK, LANES), 1) < breadth
    low_s = lax.broadcasted_iota(jnp.int32, (breadth, LANES), 1) < breadth
    head_i = lax.broadcasted_iota(jnp.int32, (LANES, LANES), 0) // breadth
    head_j = lax.broadcasted_iota(jnp.int32, (LANES, LANES), 1) // breadth
    ones = jnp.where(head_i == head_j, 1.0, 0.0).astype(BF16)
    means = jnp.where(head_i == head_j, 1.0 / breadth, 0.0).astype(BF16)

    for i in range(4):
        locals_[i].wait()
        remotes[i].wait_recv()

    def decays(q, c):
        lanes = pl.ds(pl.multiple_of(q * QUAD, QUAD), QUAD)
        states = [jnp.zeros((breadth, LANES), F32) for _ in range(2)]
        pref = jnp.zeros((1, QUAD), F32)
        for b in range(blocks):
            at = pl.ds(b * BLOCK, BLOCK)
            log_decay = -jnp.exp(fade[at, lanes].astype(F32))
            hi = log_decay.astype(BF16)
            lo = (log_decay - hi.astype(F32)).astype(BF16)
            cum = dot(incl, jnp.concatenate([hi, lo], axis=0))
            mid, total = cum[BLOCK // 2 - 1 : BLOCK // 2], cum[BLOCK - 1 :]
            km = (key[at, lanes].astype(F32) * jnp.exp(mid - cum)).astype(BF16)
            rec_mid[at, lanes] = (
                rec[at, lanes].astype(F32) * jnp.exp(cum - log_decay - mid)
            ).astype(BF16)
            key_mid[at, lanes] = km
            pref_row[b, :, lanes] = pref
            mid_row[b, :, lanes] = mid
            vb = val[at, lanes]
            end, whole = jnp.exp(total - mid), jnp.exp(total)
            for j in range(2):
                cut = slice(j * LANES, (j + 1) * LANES)
                entering[b, 2 * q + j] = states[j]
                product = dot_tn(vb[:, cut], km[:, cut])
                own = jnp.where(low_s, product[:breadth], product[breadth:])
                states[j] = states[j] * whole[:, cut] + own * end[:, cut]
            pref = pref + total
        for j in range(2):
            cut = slice(j * LANES, (j + 1) * LANES)
            for s in range(per_pair):
                slot = (2 * q + j) * per_pair + s
                outbox[slot] = states[j][s * piece : (s + 1) * piece].astype(BF16)
                outdec[slot] = pref[:, cut]
        return c

    lax.fori_loop(0, quads, decays, 0)

    inbox[me] = outbox[me]
    indec[me] = outdec[me]

    def state_copies(d):
        peer = lax.rem(me + d, n)
        return (
            pltpu.make_async_remote_copy(
                src_ref=outbox.at[peer], dst_ref=inbox.at[me],
                send_sem=s_send.at[d], recv_sem=s_recv.at[d],
                device_id=(peer, core), device_id_type=MESH,
            ),
            pltpu.make_async_remote_copy(
                src_ref=outdec.at[peer], dst_ref=indec.at[me],
                send_sem=d_send.at[d], recv_sem=d_recv.at[d],
                device_id=(peer, core), device_id_type=MESH,
            ),
        )

    def carry_copy(d):
        peer = lax.rem(me + d, n)
        return pltpu.make_async_remote_copy(
            src_ref=outbox2.at[peer], dst_ref=carry.at[me],
            send_sem=c_send.at[d], recv_sem=c_recv.at[d],
            device_id=(peer, core), device_id_type=MESH,
        )

    def send_states(d, c):
        for copy in state_copies(d):
            copy.start()
        return c

    lax.fori_loop(1, n, send_states, 0)

    def within(q, c):
        for j in range(2):
            lanes = pl.ds(pl.multiple_of(q * QUAD + j * LANES, LANES), LANES)
            reward = reward_ref[:, lanes]
            for b in range(blocks):
                at = pl.ds(b * BLOCK, BLOCK)
                vb = val[at, lanes]
                scores = dot_nt(rec_mid[at, lanes], split_heads(key_mid[at, lanes], low))
                scores = jnp.where(t_id > s_id, scores, 0.0).astype(BF16)
                own = rec[at, lanes].astype(F32) * key[at, lanes].astype(F32) * reward
                local_out[at, lanes] = dot(scores, split_heads(vb, low)) + dot(
                    own.astype(BF16), ones
                ) * vb.astype(F32)
        return c

    half = quads // 2
    lax.fori_loop(0, half, within, 0)

    def wait_states(d, c):
        for copy in state_copies(d):
            copy.wait()
        return c

    lax.fori_loop(1, n, wait_states, 0)

    def scan(i, run):
        outbox2[i] = run.astype(BF16)
        return run * jnp.exp(indec[i]) + inbox[i].astype(F32)

    lax.fori_loop(0, n, scan, jnp.zeros((piece, LANES), F32))
    carry[me] = outbox2[me]

    def send_carry(d, c):
        carry_copy(d).start()
        return c

    lax.fori_loop(1, n, send_carry, 0)
    lax.fori_loop(half, quads, within, 0)
    locals_[4].wait()
    remotes[4].wait_recv()

    def wait_carry(d, c):
        carry_copy(d).wait()
        return c

    lax.fori_loop(1, n, wait_carry, 0)

    def finish(q, c):
        for j in range(2):
            pair = 2 * q + j
            lanes = pl.ds(pl.multiple_of(q * QUAD + j * LANES, LANES), LANES)
            gain = gain_ref[:, lanes]
            came = jnp.concatenate(
                [carry[pair * per_pair + s].astype(F32) for s in range(per_pair)], axis=0
            )
            for b in range(blocks):
                at = pl.ds(b * BLOCK, BLOCK)
                state = entering[b, pair] + jnp.exp(pref_row[b, :, lanes]) * came
                state = (state * jnp.exp(mid_row[b, :, lanes])).astype(BF16)
                o = local_out[at, lanes] + dot_nt(rec_mid[at, lanes], split_heads(state, low_s))
                hi = o.astype(BF16)
                lo = (o - hi.astype(F32)).astype(BF16)
                centred = o - (dot(hi, means) + dot(lo, means))
                var = dot((centred * centred).astype(BF16), means)
                g = gate[at, lanes].astype(F32)
                normed = centred * lax.rsqrt(var + EPS) * gain
                gated[at, lanes] = (normed * (g / (1.0 + jnp.exp(-g)))).astype(BF16)
        return c

    lax.fori_loop(0, quads, finish, 0)

    def part_copy(c):
        return pltpu.make_async_remote_copy(
            src_ref=snd.at[c], dst_ref=rcv.at[c],
            send_sem=p_send.at[c], recv_sem=p_recv.at[c],
            device_id=(me, other), device_id_type=MESH,
        )

    def out_copy(c):
        return pltpu.make_async_copy(
            outv.at[c], out_hbm.at[:, pl.ds(pl.multiple_of(c * CHUNK, CHUNK), CHUNK)], o_sem.at[c]
        )

    def give(c, x):
        weight_copy(c).wait()
        snd[c] = dot(gated[their_rows, :], weight[c]).astype(BF16)
        part_copy(c).start()
        return x

    lax.fori_loop(0, chunks, give, 0)

    def take(c, x):
        mine = dot(gated[my_rows, :], weight[c])
        part_copy(c).wait_recv()
        outv[c] = (mine + rcv[c].astype(F32)).astype(BF16)
        out_copy(c).start()
        return x

    lax.fori_loop(0, chunks, take, 0)

    def drain(c, x):
        part_copy(c).wait_send()
        out_copy(c).wait()
        return x

    lax.fori_loop(0, chunks, drain, 0)
    for copy in remotes:
        copy.wait_send()


def shards(n, rec, key, val, fade, gate, reward, gain, mapping):
    rows = rec.shape[0]
    breadth = reward.shape[1]
    width = mapping.shape[0]
    depth = mapping.shape[1]
    tokens = rows * rec.shape[1] // width
    blocks, pairs, chunks = tokens // BLOCK, width // LANES, depth // CHUNK
    piece = pairs * breadth // n
    held = pltpu.VMEM((tokens, width), BF16)
    dma = pltpu.SemaphoreType.DMA
    anywhere = pl.BlockSpec(memory_space=pl.ANY)
    vmem = pl.BlockSpec(memory_space=pltpu.VMEM)
    return pl.pallas_call(
        functools.partial(kernel, n, breadth),
        out_shape=jax.ShapeDtypeStruct((rows, depth), BF16),
        in_specs=[anywhere] * 5 + [vmem] * 2 + [anywhere],
        out_specs=anywhere,
        scratch_shapes=[
            held, held, held, held, held,
            pltpu.VMEM((chunks, width, CHUNK), BF16),
            held, held,
            pltpu.VMEM((tokens, width), F32),
            pltpu.VMEM((blocks, pairs, breadth, LANES), F32),
            pltpu.VMEM((blocks, 1, width), F32),
            pltpu.VMEM((blocks, 1, width), F32),
            pltpu.VMEM((n, piece, LANES), BF16),
            pltpu.VMEM((n, 1, LANES), F32),
            pltpu.VMEM((n, piece, LANES), BF16),
            pltpu.VMEM((n, 1, LANES), F32),
            pltpu.VMEM((n, piece, LANES), BF16),
            pltpu.VMEM((n, piece, LANES), BF16),
            held,
            pltpu.VMEM((chunks, rows, CHUNK), BF16),
            pltpu.VMEM((chunks, rows, CHUNK), BF16),
            pltpu.VMEM((chunks, rows, CHUNK), BF16),
            dma((5,)), dma((5,)), dma((5,)), dma((chunks,)),
            dma((n,)), dma((n,)), dma((n,)), dma((n,)), dma((n,)), dma((n,)),
            dma((chunks,)), dma((chunks,)), dma((chunks,)),
        ],
        compiler_params=pltpu.CompilerParams(
            collective_id=0, has_side_effects=True, vmem_limit_bytes=56 * 2**20
        ),
    )(rec, key, val, fade, gate, reward.reshape(1, -1), gain.reshape(1, -1), mapping)


def solution(mesh):
    tokens = P(("seq", "head"), None)
    placed = (tokens,) * 5 + (P("head", None), P("head"), P("head", None))
    return jax.shard_map(
        functools.partial(shards, mesh.shape["seq"]),
        mesh=mesh, in_specs=placed, out_specs=tokens, check_vma=False,
    )
```

time: 255 us -> 46.1 us (0.18); the launches traced: 251 us -> 45.9 us
  waiting for transfers between devices: 50.6 us -> 0 us
  matrix products: 47.7 us -> 0 us
  blocking collectives: 44.8 us -> 0 us
  Pallas kernels: 0 us -> 41.3 us
  local copies, waits for them, and re-layouts: 45.4 us -> 4.49 us
  other arithmetic: 29.5 us -> 0 us
  starting transfers between devices: 18.7 us -> 0 us
  between operations: 14 us -> 0.01 us
    dot_general x6 -> x0, matrix products: 47.7 us -> none  [the longest x1 15.6 us: shards(): carried = jnp.einsum('ghi,ghij->hij', weights, all_state, precision=high)]
    all_gather x1 -> x0, blocking collectives: 44.8 us -> none  [shards(): lax.all_gather(device_log[None], 'seq', axis=0, tiled=True)]
    pallas_call x0 -> x1, Pallas kernels: none -> 41.3 us  [shards(): pl.pallas_call(functools.partial(kernel, n, breadth), out_shape=jax.Shape...]
    all_gather x1 -> x0, waiting for transfers between devices: 37.7 us -> none  [shards(): lax.all_gather(local_state[None], 'seq', axis=0, tiled=True)]
    convert_element_type x7 -> x0, local copies, waits for them, and re-layouts: 20.5 us -> none  [the longest x2 7.54 us: shards(): acceptance_single_real = head_major(rec_t).astype(jnp.float32)]
    all_to_all x5 -> x0, starting transfers between devices: 17.9 us -> none  [the longest x1 3.58 us: shards(): lax.all_to_all(raw_control_signal, 'head', split_axis=1, concat_axis=0, t...]
    reduce_sum x4 -> x0, other arithmetic: 10.6 us -> none  [the longest x1 9.66 us: shards(): jnp.sum(acceptance_single_real * reward * lookup_single_real, axis=-1, ke...]
    reduce_scatter x1 -> x0, waiting for transfers between devices: 10.4 us -> none  [shards(): lax.psum_scatter(jnp.dot(gated, result_mapping, preferred_element_type=jn...]
  transfers between devices with their start and end apart: 7 -> 0, of which waited for: 4 -> 0; matrix products, arithmetic and copies ran while one was open for 21% -> 0% of each run, Pallas kernels for 0% -> 0%
where the time goes in v1:
time: 46.1 us; the launch traced here: 45.9 us
  Pallas kernels  41.3 us (90%)
  local copies, waits for them, and re-layouts  4.49 us (10%)
    pallas_call x1, Pallas kernels, shards(): pl.pallas_call(functools.partial(kernel, n, breadth), out_shape=jax.Shape...  41.3 us
    unnamed x1, local copies, waits for them, and re-layouts  3.13 us
    reshape x1, local copies, waits for them, and re-layouts, shards(): reward.reshape(1, -1)  1.36 us

profile of v1, /device:TPU:0, one launch (start us, length us, event | category | flops | bytes accessed | tf_op | source)
XLA Modules:
  0.0 45.9 jit_solution(12045342408852570218)
XLA Ops:
  0.0 1.4 %reshape.6.reward_ref = f32[1,1024]{1,0:T(1,128)} reshape(f32[16,64]{1,0:T(8,128)} %param.13) | data formatting | bytes 8192 | tf_op jit(solution)/shard_map/reshape | solution.py:332
  1.4 41.3 %shard_map.82 = bf16[256,4096]{1,0:T(8,128)(2,1)} custom-call(bf16[256,2048]{1,0:T(8,128)(2,1)} %rec_hbm.1, bf16[256,2048]{1,0:T(8,128)(2,1)} %key_hbm.1, bf16[256,2048]{1,0:T(8,128)(2,1)} %val_hbm.1, bf16[256,2048]{1,0:T(8,128)(2,1)} %fade_hbm.1, bf16[256,2048]{1,0:T(8,128)(2,1)} %gate_hbm.1, f32[1,1024]{1,0:T(1,128)} %reshape.6.reward_ref, ...), custom_call_target="tpu_custom_call" | custom-call | tf_op jit(solution)/shard_map/pallas_call | solution.py:302
  42.7 3.1 %copy.10 = bf16[256,4096]{1,0:T(8,128)(2,1)} copy(bf16[256,4096]{1,0:T(8,128)(2,1)} %shard_map.82) | data formatting | bytes 4194304
